TPU v7x, 32 devices: a whole 2x2x4 slice. The times are simulated.
32 devices in a mesh: seq: 8 (over y, x, core), batch: 4 (over z).
Axes of the slice: x: 2, y: 2, z: 4, core: 2. Of those that a mesh axis runs over, the one named last changes fastest.
Arguments:
- query_rows: bfloat16 [4, 1024, 2048], P('batch', 'seq'), may hold values from -6 to 6, as said below
- key_rows: bfloat16 [4, 1024, 1024], P('batch', 'seq'), may hold values from -6 to 6, as said below
- value_rows: bfloat16 [4, 1024, 1024], P('batch', 'seq'), may hold values from -6 to 6, as said below
- attn_output: bfloat16 [4, 1024, 2048], P('batch', 'seq'), may hold values from -6 to 6, as said below
- output_grad: bfloat16 [4, 1024, 2048], P('batch', 'seq'), may hold values from -6 to 6
- log_norm: float32 [4, 16, 1024], P('batch', None, 'seq'), as said below
- slab_order: int32 [4, 8], P('batch', 'seq'), may hold values from 0 to 7, as said below
- normed_input: bfloat16 [4, 1024, 4608], P('batch', 'seq'), may hold values from -6 to 6
Outputs:
- grad_query: bfloat16 [4, 1024, 2048], P('batch', 'seq')
- grad_key: bfloat16 [4, 1024, 1024], P('batch', 'seq')
- grad_weight: float32 [4608, 1024], P('seq')
Inputs may be any that keep to these rules, and one draw needn't show every extreme that they name: `query_rows`: queries of a causal forward pass with 16 heads. `key_rows`: keys of the same forward pass with 8 heads. `value_rows`: values of the same forward pass. `attn_output`: the forward pass's output: for each head, sum over keys at or before the query's position of exp(score - log_norm) times the value. `log_norm`: log of the sum of exp(score) over the keys at or before the query's position, so that each row's weights sum to one. `slab_order`: each row is a permutation of the slab places.
All inputs are finite; a program needn't handle non-finite values.
Results may differ from a plain program's by a relative error of at most 0.025.
Values may be sent and summed in bfloat16 or wider, within the bound.
A program may use at most 128 MiB of HBM per device.

v0:
```python
import jax
import jax.numpy as jnp
from jax import lax
from jax.sharding import PartitionSpec as P

HEADS = 16
KV_HEADS = 8
HEAD = 128


SCALE = 144.0 ** (-0.5)


def block_terms(queries, grads, delta, norms, query_pos, key_block, value_block, key_pos):
    keys_count = key_block.shape[0]
    scores = SCALE * jnp.einsum(
        "tgrd,kgd->grtk", queries, key_block, preferred_element_type=jnp.float32
    )
    allowed = key_pos[None, :] <= query_pos[:, None]
    probs = jnp.where(allowed, jnp.exp(scores - norms[..., None]), 0.0)
    dprob = jnp.einsum("tgrd,kgd->grtk", grads, value_block, preferred_element_type=jnp.float32)
    dscore = probs * (dprob - delta[..., None])
    probs_low = probs.astype(jnp.bfloat16)
    dscore_low = dscore.astype(jnp.bfloat16)
    grad_q = SCALE * jnp.einsum(
        "grtk,kgd->tgrd", dscore_low, key_block, preferred_element_type=jnp.float32
    )
    grad_k = SCALE * jnp.einsum(
        "grtk,tgrd->kgd", dscore_low, queries, preferred_element_type=jnp.float32
    )
    grad_v = jnp.einsum("grtk,tgrd->kgd", probs_low, grads, preferred_element_type=jnp.float32)
    return (grad_q, grad_k.reshape(keys_count, -1), grad_v.reshape(keys_count, -1))


def local(
    query_rows, key_rows, value_rows, attn_output, output_grad, log_norm, slab_order, normed_input
):
    tokens = query_rows.shape[1]
    group = HEADS // KV_HEADS
    kv_width = KV_HEADS * HEAD
    slabs = lax.axis_size("seq")
    length = tokens * slabs
    orders = lax.all_gather(slab_order, "seq", axis=1, tiled=True)
    queries = query_rows[0].reshape(tokens, KV_HEADS, group, HEAD)
    grads = output_grad[0].reshape(tokens, KV_HEADS, group, HEAD)
    outputs = attn_output[0].reshape(tokens, KV_HEADS, group, HEAD)
    delta = jnp.transpose(
        jnp.sum(grads.astype(jnp.float32) * outputs.astype(jnp.float32), axis=3), (1, 2, 0)
    )
    norms = log_norm[0].reshape(KV_HEADS, group, tokens)
    offsets = jnp.arange(tokens, dtype=jnp.int32)
    query_pos = slab_order[0, 0] * tokens + offsets
    width = tokens * -(-512 // tokens)
    empty_kv = jnp.zeros((length, kv_width), jnp.float32)
    empty_q = jnp.zeros((tokens, KV_HEADS, group, HEAD), jnp.float32)
    start = jnp.int32(0)
    grad_q = empty_q
    grad_k = empty_kv
    grad_v = empty_kv
    key_part = lax.all_gather(key_rows, "seq", axis=1, tiled=True)
    value_part = lax.all_gather(value_rows, "seq", axis=1, tiled=True)
    count = key_part.shape[1]
    for begin in range(0, count, width):
        finish = min(begin + width, count)
        shards = (finish - begin) // tokens
        first = (start + begin) // tokens
        places = lax.dynamic_slice_in_dim(orders[0], first, shards, 0)
        key_pos = (places[:, None] * tokens + offsets[None, :]).reshape(-1)
        key_block = key_part[0, begin:finish].reshape(-1, KV_HEADS, HEAD)
        value_block = value_part[0, begin:finish].reshape(-1, KV_HEADS, HEAD)
        term_q, term_k, term_v = block_terms(
            queries, grads, delta, norms, query_pos, key_block, value_block, key_pos
        )
        grad_q = grad_q + term_q
        grad_k = lax.dynamic_update_slice_in_dim(grad_k, term_k, begin, 0)
        grad_v = lax.dynamic_update_slice_in_dim(grad_v, term_v, begin, 0)
    grad_q, part_key, part_value = (grad_q, grad_k, grad_v)
    key_sum, value_sum = (
        lax.psum_scatter(
            part_key.astype(jnp.bfloat16), "seq", scatter_dimension=0, tiled=True
        ).astype(jnp.float32),
        lax.psum_scatter(
            part_value.astype(jnp.bfloat16), "seq", scatter_dimension=0, tiled=True
        ).astype(jnp.float32),
    )
    every_grad = lax.all_gather(value_sum.astype(jnp.bfloat16), "seq", axis=0, tiled=True)
    own_columns = lax.all_to_all(normed_input[0], "seq", split_axis=1, concat_axis=0, tiled=True)
    share = own_columns.shape[1]
    slab_parts = jnp.einsum(
        "std,stk->sdk",
        own_columns.reshape(slabs, tokens, share),
        every_grad.reshape(slabs, tokens, kv_width),
        preferred_element_type=jnp.float32,
    )
    rows_total = jnp.sum(slab_parts.astype(jnp.bfloat16).astype(jnp.float32), axis=0)
    weight = lax.psum(rows_total.astype(jnp.bfloat16), "batch").astype(jnp.float32)
    grad_query = grad_q.astype(jnp.bfloat16).reshape(1, tokens, HEADS * HEAD)
    grad_key = key_sum.astype(jnp.bfloat16).reshape(1, tokens, kv_width)
    return (grad_query, grad_key, weight)


def solution(mesh):
    placed = (
        P("batch", "seq", None),
        P("batch", "seq", None),
        P("batch", "seq", None),
        P("batch", "seq", None),
        P("batch", "seq", None),
        P("batch", None, "seq"),
        P("batch", "seq"),
        P("batch", "seq", None),
    )
    return jax.shard_map(
        local,
        mesh=mesh,
        in_specs=placed,
        out_specs=(P("batch", "seq", None), P("batch", "seq", None), P("seq", None)),
        check_vma=False,
    )
```

profile of v0, /device:TPU:0, one launch (start us, length us, event | category | flops | bytes accessed | tf_op | source)
XLA Modules:
  0.0 277.6 jit_solution(16221604361421081299)
XLA Ops:
  7.2 0.0 all-gather.4.cloned.1.call-start
  7.2 1.8 copy.57
  9.1 0.0 all-gather.4.cloned.1.call-update
  9.1 0.0 reduce-scatter.7.cloned.1.call-start
  9.8 1.2 dynamic-slice.2
  11.0 0.7 bitcast_dynamic-update-slice_fusion
  11.7 9.5 %all-reduce = s32[8]{0:T(128)S(1)} all-reduce(s32[8]{0:T(128)S(1)} %bitcast_dynamic-update-slice_fusion), channel_id=1, replica_groups=mesh['seq'=8,'batch'=4] {'seq'}, use_global_device_ids=true, to_apply=%add | all-reduce | flops 8 | bytes 64
  21.2 1.4 reshape_squeeze.22
  22.6 1.2 copy.77
  23.8 0.0 copy-done.5
  23.8 0.3 copy.109
  24.1 0.1 multiply_bitcast_fusion
  24.2 0.1 add_bitcast_fusion
  24.2 0.2 broadcast_compare_fusion
  24.5 16.8 %all-gather.4.cloned.1.call-done = bf16[1,1024,1024]{1,2,0:T(8,128)(2,1)} async-done(((bf16[1,128,1024]{1,2,0:T(8,128)(2,1)}), bf16[1,1024,1024]{1,2,0:T(8,128)(2,1)}) %all-gather.4.cloned.1.call-update) | async-done | bytes 2097168 | tf_op jit(solution)/shard_map/all_gather | solution.py:60
  41.3 1.7 fusion.36
  43.0 0.8 fusion.38
  43.8 0.0 copy-start.6
  43.8 0.0 copy-start.9
  43.8 0.8 fusion.37
  44.5 1.2 copy-done.3
  45.7 1.0 bitcast_convert_fusion
  46.7 0.2 copy-done.2
  47.0 1.0 bitcast_convert_fusion.1
  47.9 1.6 pad_maximum_fusion.1
  49.6 4.0 %copy.107 = bf16[1024,1024]{1,0:T(8,128)(2,1)} copy(bf16[1024,1024]{0,1:T(8,128)(2,1)} %pad_maximum_fusion.1) | data formatting | bytes 4194304
  53.6 0.0 reduce-scatter.7.cloned.1.call-update
  53.6 0.0 all-gather.6.cloned.1.call-start
  53.6 0.8 copy.60
  54.5 0.0 all-gather.6.cloned.1.call-update
  54.5 0.0 all-gather.8.cloned.1.call-start
  54.6 40.3 %reduce-scatter.7.cloned.1.call-done = bf16[128,1024]{1,0:T(8,128)(2,1)} async-done(((bf16[1024,1024]{1,0:T(8,128)(2,1)}), bf16[128,1024]{1,0:T(8,128)(2,1)}) %reduce-scatter.7.cloned.1.call-update) | async-done | bytes 262160
  94.8 1.8 copy.108
  96.6 0.0 all-gather.8.cloned.1.call-update
  96.7 2.4 copy.81
  99.1 4.3 %all-to-all-start = ((bf16[128,8,576]{0,2,1:T(8,128)(2,1)}), bf16[128,8,576]{0,2,1:T(8,128)(2,1)}, u32[]{:S(2)}, u32[]{:S(2)}) async-start(bf16[128,8,576]{0,2,1:T(8,128)(2,1)} %bitcast.146), calls=%async_computation.1 | async-start | bytes 2359296 | tf_op jit(solution)/shard_map/all_to_all | solution.py:87
  103.3 0.2 all-reduce.3.cloned.1.call-start
  103.5 3.1 %reshape.104 = f32[128,8,2,128]{3,2,1,0:T(2,128)} reshape(bf16[1,128,2048]{2,1,0:T(8,128)(2,1)} %param.11) | data formatting | bytes 1572864 | tf_op jit(solution)/shard_map/convert_element_type | solution.py:48
  106.6 3.2 %multiply_reduce_fusion = f32[128,8,2]{2,1,0:T(8,128)} fusion(f32[128,8,2,128]{3,2,1,0:T(2,128)} %reshape.104, bf16[128,8,2,128]{3,2,1,0:T(2,128)(2,1)S(1)} %reshape_squeeze.22), kind=kLoop, calls=%fused_computation.37 | loop fusion | flops 784384 | bytes 1581056 | tf_op jit(solution)/shard_map/reduce_sum | solution.py:48
  109.9 1.3 copy.63
  111.1 19.6 %all-gather.6.cloned.1.call-done = bf16[1,1024,1024]{1,2,0:T(8,128)(2,1)} async-done(((bf16[1,128,1024]{1,2,0:T(8,128)(2,1)}), bf16[1,1024,1024]{1,2,0:T(8,128)(2,1)}) %all-gather.6.cloned.1.call-update) | async-done | bytes 2097168 | tf_op jit(solution)/shard_map/all_gather | solution.py:61
  130.7 2.8 %fusion.35 = (bf16[1,512,1024]{1,2,0:T(8,128)(2,1)S(1)}, bf16[1,512,1024]{1,2,0:T(8,128)(2,1)}) fusion(bf16[1,1024,1024]{1,2,0:T(8,128)(2,1)} %all-gather.6.cloned.1.call-done), kind=kLoop, calls=%fused_computation.50 | loop fusion | bytes 4194304 | tf_op jit(solution)/shard_map/slice | solution.py:70
  133.5 0.1 copy-done.4
  133.6 2.9 %fusion.1 = bf16[8,2,128,512]{2,3,1,0:T(8,128)(2,1)} fusion(f32[8,512,128,2]{2,1,3,0:T(8,128)S(1)} %copy-done.4, bf16[512,8,128,1]{0,2,3,1:T(8,128)(2,1)S(1)} %bitcast.154, bf16[128,8,2,128]{0,3,2,1:T(8,128)(2,1)S(1)} %copy-done.7, f32[8,2,128]{2,1,0:T(2,128)S(1)} %copy.63, f32[8,2,128]{2,1,0:T(2,128)S(1)} %bitcast.161, ...), kind=kOutput, calls=%fused_computation.3 | convolution fusion | flops 274726912 | bytes 7946240 | tf_op jit(solution)/shard_map/tgrd,kgd->grtk/dot_general | solution.py:21
  136.5 24.1 %all-gather.8.cloned.1.call-done = bf16[1024,1024]{0,1:T(8,128)(2,1)} async-done(((bf16[128,1024]{0,1:T(8,128)(2,1)}), bf16[1024,1024]{0,1:T(8,128)(2,1)}) %all-gather.8.cloned.1.call-update) | async-done | bytes 2097168 | tf_op jit(solution)/shard_map/all_gather | solution.py:86
  160.6 3.9 %copy.80 = bf16[1024,1024]{1,0:T(8,128)(2,1)} copy(bf16[1024,1024]{0,1:T(8,128)(2,1)} %all-gather.8.cloned.1.call-done) | data formatting | bytes 4194304 | tf_op jit(solution)/shard_map/all_gather | solution.py:86
  164.5 0.0 all-to-all-done
  164.5 5.8 %convert_reduce_fusion = bf16[1024,576]{0,1:T(8,128)(2,1)} fusion(bf16[8,128,1024]{2,1,0:T(8,128)(2,1)} %bitcast.150, bf16[128,8,576]{0,2,1:T(8,128)(2,1)} %all-to-all-done), kind=kOutput, calls=%fused_computation | convolution fusion | flops 1216806912 | bytes 4456448 | tf_op jit(solution)/shard_map/std,stk->sdk/dot_general | solution.py:89
  170.3 0.0 all-reduce.3.cloned.1.call-update
  170.4 0.0 reduce-scatter.5.cloned.1.call-start
  170.4 3.4 %fusion.14 = bf16[8,512,128]{1,2,0:T(8,128)(2,1)} fusion(bf16[8,2,128,512]{2,3,1,0:T(8,128)(2,1)} %fusion.1, bf16[128,8,2,128]{0,3,2,1:T(8,128)(2,1)S(1)} %bitcast.140), kind=kOutput, calls=%fused_computation.22 | convolution fusion | flops 269484032 | bytes 3670016 | tf_op jit(solution)/shard_map/grtk,tgrd->kgd/dot_general | solution.py:28
  173.8 2.3 copy.75
  176.1 4.0 %fusion.5 = bf16[8,2,128,512]{2,3,1,0:T(8,128)(2,1)S(1)} fusion(f32[8,512,128,2]{2,1,3,0:T(8,128)} %copy-done.2, bf16[512,8,128,1]{0,2,3,1:T(8,128)(2,1)} %bitcast.153, bf16[128,8,2,128]{0,3,2,1:T(8,128)(2,1)S(1)} %copy-done.7, f32[8,2,128]{2,1,0:T(2,128)S(1)} %copy.63, f32[8,2,128]{2,1,0:T(2,128)S(1)} %bitcast.162, pred[128,512]{0,1:T(8,128)(4,1)S(1)} %get-tuple-element.17), kind=kOutput, calls=%fused_computation.9 | convolution fusion | flops 274726912 | bytes 7946240 | tf_op jit(solution)/shard_map/tgrd,kgd->grtk/dot_general | solution.py:21
  180.0 0.0 copy-start.1
  180.1 1.8 fusion.15
  181.9 2.3 copy.74
  184.2 3.1 %pad_maximum_fusion = bf16[1024,1024]{1,0:T(8,128)(2,1)} fusion(bf16[512,1024]{1,0:T(8,128)(2,1)} %copy.75, bf16[512,1024]{1,0:T(8,128)(2,1)} %copy.74), kind=kLoop, calls=%fused_computation.17 | loop fusion | flops 4194304 | bytes 4194304 | tf_op jit(solution)/shard_map/dynamic_update_slice | solution.py:75
  187.2 0.0 reduce-scatter.5.cloned.1.call-update
  187.3 2.3 fusion.39
  189.5 0.6 fusion.29
  190.1 1.0 copy.82
  191.1 35.4 %all-reduce.3.cloned.1.call-done = bf16[576,1024]{1,0:T(8,128)(2,1)} async-done(((bf16[576,1024]{1,0:T(8,128)(2,1)}), bf16[576,1024]{1,0:T(8,128)(2,1)}) %all-reduce.3.cloned.1.call-update) | async-done | bytes 1179664 | tf_op jit(solution)/shard_map/psum | solution.py:96
  226.5 3.0 %convert_element_type.60 = f32[576,1024]{1,0:T(8,128)} convert(bf16[576,1024]{1,0:T(8,128)(2,1)} %all-reduce.3.cloned.1.call-done) | non-fusion elementwise | flops 589824 | bytes 3538944 | tf_op jit(solution)/shard_map/convert_element_type | solution.py:96
  229.5 41.3 %reduce-scatter.5.cloned.1.call-done = bf16[128,1024]{1,0:T(8,128)(2,1)} async-done(((bf16[1024,1024]{1,0:T(8,128)(2,1)}), bf16[128,1024]{1,0:T(8,128)(2,1)}) %reduce-scatter.5.cloned.1.call-update) | async-done | bytes 262160 | tf_op jit(solution)/shard_map/reduce_scatter | solution.py:79
  (15 shorter events, 0.0 us)
Async XLA Ops:
  7.2 16.6 %copy-start.5 = (bf16[1,128,2048]{2,1,0:T(8,128)(2,1)S(1)}, bf16[1,128,2048]{2,1,0:T(8,128)(2,1)}, u32[]{:S(2)}) copy-start(bf16[1,128,2048]{2,1,0:T(8,128)(2,1)} %param.8) | copy-start | bytes 1572868
  7.2 34.1 %all-gather.4.cloned.1.call-start = ((), (), s32[]{:S(2)}) async-start(), calls=%async_computation.3 | async-start | bytes 2359296 | tf_op jit(solution)/shard_map/all_gather | solution.py:60
  9.1 85.8 %reduce-scatter.7.cloned.1.call-start = ((), (), s32[]{:S(2)}) async-start(), calls=%async_computation.8 | async-start | bytes 2359296
  43.7 2.0 copy-start.3
  43.8 2.0 copy-start.6
  43.8 2.0 copy-start.9
  44.5 2.4 copy-start.2
  49.6 4.1 %copy-start.8 = (bf16[1,128,1024]{2,1,0:T(8,128)(2,1)S(1)}, bf16[1,128,1024]{2,1,0:T(8,128)(2,1)}, u32[]{:S(2)}) copy-start(bf16[1,128,1024]{2,1,0:T(8,128)(2,1)} %param.10) | copy-start | bytes 786436
  53.6 77.1 %all-gather.6.cloned.1.call-start = ((), (), s32[]{:S(2)}) async-start(), calls=%async_computation.4 | async-start | bytes 2359296 | tf_op jit(solution)/shard_map/all_gather | solution.py:61
  54.5 106.0 %all-gather.8.cloned.1.call-start = ((), (), s32[]{:S(2)}) async-start(), calls=%async_computation.6 | async-start | bytes 2359296 | tf_op jit(solution)/shard_map/all_gather | solution.py:86
  99.1 65.4 %all-to-all-start = ((bf16[128,8,576]{0,2,1:T(8,128)(2,1)}), bf16[128,8,576]{0,2,1:T(8,128)(2,1)}, u32[]{:S(2)}, u32[]{:S(2)}) async-start(bf16[128,8,576]{0,2,1:T(8,128)(2,1)} %bitcast.146), calls=%async_computation.1 | async-start | bytes 2359296 | tf_op jit(solution)/shard_map/all_to_all | solution.py:87
  103.3 123.2 %all-reduce.3.cloned.1.call-start = ((), (), s32[]{:S(2)}) async-start(), calls=%async_computation.7 | async-start | bytes 2359296 | tf_op jit(solution)/shard_map/psum | solution.py:96
  109.9 23.7 %copy-start.7 = (bf16[128,8,2,128]{0,3,2,1:T(8,128)(2,1)S(1)}, bf16[128,8,2,128]{0,3,2,1:T(8,128)(2,1)}, u32[]{:S(2)}) copy-start(bf16[128,8,2,128]{0,3,2,1:T(8,128)(2,1)} %copy.77) | copy-start | bytes 1572868
  130.7 2.9 %copy-start.4 = (f32[8,512,128,2]{2,1,3,0:T(8,128)S(1)}, f32[8,512,128,2]{2,1,3,0:T(8,128)}, u32[]{:S(2)}) copy-start(f32[8,512,128,2]{2,1,3,0:T(8,128)} %copy-done.3) | copy-start | bytes 12582916
  170.4 100.4 %reduce-scatter.5.cloned.1.call-start = ((), (), s32[]{:S(2)}) async-start(), calls=%async_computation.5 | async-start | bytes 2359296 | tf_op jit(solution)/shard_map/reduce_scatter | solution.py:79
  180.0 1.8 copy-start.1
  187.3 2.3 copy-start
Sparse Core Ops, SparseCore 0:
  10.4 30.8 all-gather.3
  53.7 41.0 reduce-scatter.6
  97.3 33.3 all-gather.5
  132.4 28.0 all-gather.7
  170.5 55.9 all-reduce.2
  230.2 40.5 reduce-scatter.4
where the time goes:
time: 278 us
  waiting for transfers between devices  178 us (64%)
  local copies, waits for them, and re-layouts  35.5 us (13%)
  matrix products  24.2 us (9%)
  between operations  14.9 us (5%)
  other arithmetic  11.3 us (4%)
  blocking collectives  9.51 us (3%)
  starting transfers between devices  4.68 us (2%)
    reduce_scatter x1, waiting for transfers between devices, local(): lax.psum_scatter(part_key.astype(jnp.bfloat16), 'seq', scatter_dimension=...  41.3 us
    unnamed x7, waiting for transfers between devices  40.4 us
    psum x1, waiting for transfers between devices, local(): lax.psum(rows_total.astype(jnp.bfloat16), 'batch').astype(jnp.float32)  35.4 us
    all_gather x1, waiting for transfers between devices, local(): lax.all_gather(value_sum.astype(jnp.bfloat16), 'seq', axis=0, tiled=True)  24.1 us
    all_gather x1, waiting for transfers between devices, local(): value_part = lax.all_gather(value_rows, 'seq', axis=1, tiled=True)  19.6 us
    all_gather x1, waiting for transfers between devices, local(): key_part = lax.all_gather(key_rows, 'seq', axis=1, tiled=True)  16.8 us
    unnamed x29, local copies, waits for them, and re-layouts  15.3 us
    unnamed x1, blocking collectives  9.51 us
  transfers between devices with their start and end apart: 7, of which 6 were waited for; matrix products, arithmetic and copies ran while one was open for 18% of the time, Pallas kernels for 0%

commit v1 on v0

--- a/solution.py
+++ b/solution.py
@@ -1,6 +1,11 @@
+import functools
+import math
+
 import jax
 import jax.numpy as jnp
 from jax import lax
+from jax.experimental import pallas as pl
+from jax.experimental.pallas import tpu as pltpu
 from jax.sharding import PartitionSpec as P
 
 HEADS = 16
@@ -99,6 +104,365 @@
     return (grad_query, grad_key, weight)
 
 
+MESH = pl.DeviceIdType.MESH
+F32 = jnp.float32
+BF16 = jnp.bfloat16
+NT = (((1,), (1,)), ((), ()))
+
+
+def xor(a, b, n):
+    out = 0
+    bit = 1
+    while bit < n:
+        x, y = lax.rem(lax.div(a, bit), 2), lax.rem(lax.div(b, bit), 2)
+        out = out + bit * (x + y - 2 * x * y)
+        bit *= 2
+    return out
+
+
+def at(seq, batch):
+    return {"seq": seq, "batch": batch}
+
+
+def window(width, n):
+    share = width // n
+    step = math.gcd(share, 128)
+    return share, -(-(128 - step + share) // 128) * 128
+
+
+def kernel(
+    n, nb, q_ref, k_ref, v_ref, o_ref, g_ref, norm_ref, order_ref, x_ref,
+    gq_ref, gk_ref, gw_ref,
+    qr, gr, kr, vr, xr, st_src, str_, kt, xt, dk_acc, dv_acc, dq_buf, dk_buf, dv_all,
+    prod, up, cr, snd, tot, gq_in, gk_in,
+    in_send, in_recv, out_send, out_recv, zu_send, zu_recv, zc_recv, zd_send,
+):
+    me = lax.axis_index("seq")
+    b = lax.axis_index("batch")
+    T = k_ref.shape[0]
+    H = HEAD
+    R = HEADS // KV_HEADS
+    share, win = window(x_ref.shape[1], n)
+    half = nb // 2
+    left = b < half
+    is_end = jnp.logical_or(b == 0, b == nb - 1)
+    is_mid = jnp.logical_or(b == half - 1, b == half)
+    not_end = jnp.logical_not(is_end)
+    not_mid = jnp.logical_not(is_mid)
+    inner = jnp.where(left, b + 1, b - 1)
+    outer = jnp.where(is_end, inner, jnp.where(left, b - 1, b + 1))
+
+    barrier = pltpu.get_barrier_semaphore()
+    for t in range(1, n):
+        pl.semaphore_signal(barrier, inc=1, device_id=at(xor(me, jnp.int32(t), n), b), device_id_type=MESH)
+    pl.semaphore_signal(barrier, inc=1, device_id=at(me, inner), device_id_type=MESH)
+
+    @pl.when(not_end)
+    def _():
+        pl.semaphore_signal(barrier, inc=1, device_id=at(me, outer), device_id_type=MESH)
+
+    pl.semaphore_wait(barrier, jnp.where(is_end, n, n + 1))
+
+    def cols(who, width):
+        return pl.ds(pl.multiple_of(who * width, 128), width)
+
+    def xstart(who):
+        return pl.multiple_of(lax.div(who * share, 128) * 128, 128)
+
+    def send_in(kind, t):
+        peer = xor(me, jnp.int32(t), n)
+        src, dst = {
+            0: lambda: (k_ref.at[:, cols(peer, H)], kr.at[me]),
+            1: lambda: (v_ref.at[:, cols(peer, H)], vr.at[me]),
+            2: lambda: (q_ref.at[:, cols(peer, R * H)], qr.at[me]),
+            3: lambda: (g_ref.at[:, cols(peer, R * H)], gr.at[me]),
+            4: lambda: (x_ref.at[:, pl.ds(xstart(peer), win)], xr.at[me]),
+            5: lambda: (st_src.at[peer], str_.at[me]),
+        }[kind]()
+        return pltpu.make_async_remote_copy(
+            src_ref=src, dst_ref=dst, send_sem=in_send.at[kind, t], recv_sem=in_recv.at[kind, t],
+            device_id=at(peer, b), device_id_type=MESH)
+
+    def send_out(kind, t):
+        peer = xor(me, jnp.int32(t), n)
+        src, dst = {
+            0: lambda: (dv_all.at[me], dv_all.at[me]),
+            1: lambda: (dk_buf.at[peer], gk_in.at[me]),
+            2: lambda: (dq_buf.at[peer], gq_in.at[me]),
+        }[kind]()
+        return pltpu.make_async_remote_copy(
+            src_ref=src, dst_ref=dst, send_sem=out_send.at[kind, t], recv_sem=out_recv.at[kind, t],
+            device_id=at(peer, b), device_id_type=MESH)
+
+    for kind in (0, 1):
+        for t in range(1, n):
+            send_in(kind, t).start()
+    for t in range(1, n):
+        send_in(2, t).start()
+        send_in(3, t).start()
+
+    lane = lax.broadcasted_iota(jnp.int32, (T, 128), 1)
+    table = jnp.zeros((T, 128), F32)
+    for h in range(HEADS):
+        part = g_ref[:, h * H:(h + 1) * H].astype(F32) * o_ref[:, h * H:(h + 1) * H].astype(F32)
+        table = jnp.where(lane == h, jnp.sum(part, axis=1, keepdims=True), table)
+    delta = jnp.transpose(table)
+    base = jnp.full((8 - 2 * R, T), (order_ref[0, 0] * T).astype(F32))
+    for h in range(n):
+        st_src[h, 0:R, :] = norm_ref[h * R:(h + 1) * R, :]
+        st_src[h, R:2 * R, :] = delta[h * R:(h + 1) * R, :]
+        st_src[h, 2 * R:8, :] = base
+    for t in range(1, n):
+        send_in(5, t).start()
+    for t in range(1, n):
+        send_in(4, t).start()
+
+    kr[me] = k_ref[:, cols(me, H)]
+    vr[me] = v_ref[:, cols(me, H)]
+    qr[me] = q_ref[:, cols(me, R * H)]
+    gr[me] = g_ref[:, cols(me, R * H)]
+    xr[me] = x_ref[:, pl.ds(xstart(me), win)]
+    str_[me] = st_src[me]
+    dk_acc[...] = jnp.zeros_like(dk_acc)
+    dv_acc[...] = jnp.zeros_like(dv_acc)
+
+    for t in range(1, n):
+        for kind in (0, 1, 5):
+            send_in(kind, t).wait_recv()
+    for s in range(n):
+        kt[:, s * T:(s + 1) * T] = jnp.transpose(kr[s])
+
+    pair = 2 if n % 2 == 0 else 1
+    rows = lax.broadcasted_iota(jnp.int32, (T, R * T), 0).astype(F32)
+    qoff = lax.broadcasted_iota(jnp.int32, (1, T), 1).astype(F32)
+
+    def wide(i, first):
+        return jnp.concatenate([str_[i, first + r:first + r + 1, :] for r in range(R)], axis=1)
+
+    def per_query(t, carry):
+        i = xor(me, t, n)
+
+        @pl.when(t > 0)
+        def _():
+            send_in(2, t).wait_recv()
+            send_in(3, t).wait_recv()
+
+        qb, gb = qr[i], gr[i]
+        qs = jnp.concatenate([qb[:, r * H:(r + 1) * H] for r in range(R)], axis=0)
+        gs = jnp.concatenate([gb[:, r * H:(r + 1) * H] for r in range(R)], axis=0)
+        norms, deltas = wide(i, 0), wide(i, R)
+        qpos = str_[i, 2 * R:2 * R + 1, :] + qoff
+        qpos = jnp.concatenate([qpos] * R, axis=1)
+        dqt = jnp.zeros((H, R * T), F32)
+        for s in range(0, n, pair):
+            kb = kr[s:s + pair].reshape(pair * T, H)
+            vb = vr[s:s + pair].reshape(pair * T, H)
+            kpos = jnp.concatenate(
+                [rows + jnp.concatenate([str_[s + p, 2 * R:2 * R + 1, :]] * R, axis=1) for p in range(pair)],
+                axis=0)
+            scores = SCALE * lax.dot_general(kb, qs, NT, preferred_element_type=F32)
+            probs = jnp.where(kpos <= qpos, jnp.exp(scores - norms), 0.0)
+            dprob = lax.dot_general(vb, gs, NT, preferred_element_type=F32)
+            low = (probs * (dprob - deltas)).astype(BF16)
+            span = slice(s * T, (s + pair) * T)
+            dv_acc[span, :] += jnp.dot(probs.astype(BF16), gs, preferred_element_type=F32)
+            dk_acc[span, :] += jnp.dot(low, qs, preferred_element_type=F32)
+            dqt = dqt + jnp.dot(kt[:, span], low, preferred_element_type=F32)
+        dq = jnp.transpose(dqt * SCALE)
+        for r in range(R):
+            dq_buf[i, :, r * H:(r + 1) * H] = dq[r * T:(r + 1) * T, :].astype(BF16)
+        return carry
+
+    lax.fori_loop(0, n, per_query, 0)
+
+    dv_all[me] = dv_acc[...].astype(BF16)
+    for t in range(1, n):
+        send_out(0, t).start()
+    dk_buf[...] = (dk_acc[...] * SCALE).astype(BF16).reshape(dk_buf.shape)
+    for kind in (1, 2):
+        for t in range(1, n):
+            send_out(kind, t).start()
+
+    def turn(t, carry):
+        i = xor(me, t, n)
+
+        @pl.when(t > 0)
+        def _():
+            send_in(4, t).wait_recv()
+
+        xt[:, pl.ds(pl.multiple_of(i * T, 128), T)] = jnp.transpose(xr[i])
+        return carry
+
+    lax.fori_loop(0, n, turn, 0)
+
+    off = pl.multiple_of(me * share - xstart(me), math.gcd(share, 128))
+
+    def cross(c):
+        return pltpu.make_async_remote_copy(
+            src_ref=snd.at[c], dst_ref=cr.at[c], send_sem=zu_send.at[c], recv_sem=zc_recv.at[c],
+            device_id=at(me, inner), device_id_type=MESH)
+
+    def inward(c):
+        return pltpu.make_async_remote_copy(
+            src_ref=snd.at[c], dst_ref=up.at[c], send_sem=zu_send.at[c], recv_sem=zu_recv.at[c],
+            device_id=at(me, inner), device_id_type=MESH)
+
+    def outward(c):
+        return pltpu.make_async_remote_copy(
+            src_ref=tot.at[c], dst_ref=cr.at[c], send_sem=zd_send.at[c], recv_sem=zc_recv.at[c],
+            device_id=at(me, outer), device_id_type=MESH)
+
+    def go_up(c):
+        @pl.when(c > 0)
+        def _():
+            send_out(0, c).wait_recv()
+
+        prod[...] = jnp.dot(xt[...], dv_all[xor(me, c, n)], preferred_element_type=F32)
+
+        @pl.when(is_end)
+        def _():
+            snd[c] = prod[pl.ds(off, share), :].astype(BF16)
+
+        @pl.when(not_end)
+        def _():
+            inward(c).wait_recv()
+            snd[c] = (prod[pl.ds(off, share), :] + up[c].astype(F32)).astype(BF16)
+
+        @pl.when(is_mid)
+        def _():
+            cross(c).start()
+
+        @pl.when(not_mid)
+        def _():
+            inward(c).start()
+
+    def go_down(c):
+        cross(c).wait_recv()
+        head = cols(xor(me, c, n), H)
+
+        @pl.when(is_mid)
+        def _():
+            tot[c] = (snd[c].astype(F32) + cr[c].astype(F32)).astype(BF16)
+
+        @pl.when(not_mid)
+        def _():
+            tot[c] = cr[c]
+
+        @pl.when(not_end)
+        def _():
+            outward(c).start()
+
+        gw_ref[:, head] = tot[c].astype(F32)
+
+    lag = 2
+
+    def z_step(c, carry):
+        @pl.when(c < n)
+        def _():
+            go_up(c)
+
+        @pl.when(c >= lag)
+        def _():
+            go_down(c - lag)
+
+        return carry
+
+    lax.fori_loop(0, n + lag, z_step, 0)
+
+    gk_ref[:, cols(me, H)] = dk_buf[me]
+    gq_ref[:, cols(me, R * H)] = dq_buf[me]
+
+    def collect(t, carry):
+        i = xor(me, t, n)
+        send_out(1, t).wait_recv()
+        send_out(2, t).wait_recv()
+        gk_ref[:, cols(i, H)] = gk_in[i]
+        gq_ref[:, cols(i, R * H)] = gq_in[i]
+        return carry
+
+    lax.fori_loop(1, n, collect, 0)
+
+    def drain(t, carry):
+        for kind in range(6):
+            send_in(kind, t).wait_send()
+        for kind in range(3):
+            send_out(kind, t).wait_send()
+        return carry
+
+    lax.fori_loop(1, n, drain, 0)
+
+    def drain_z(c, carry):
+        cross(c).wait_send()
+
+        @pl.when(not_end)
+        def _():
+            outward(c).wait_send()
+
+        return carry
+
+    lax.fori_loop(0, n, drain_z, 0)
+
+
+def by_heads(
+    n, nb, query_rows, key_rows, value_rows, attn_output, output_grad, log_norm, slab_order, normed_input
+):
+    T = query_rows.shape[1]
+    H = HEAD
+    R = HEADS // KV_HEADS
+    L = n * T
+    share, win = window(normed_input.shape[2], n)
+    vm = pl.BlockSpec(memory_space=pltpu.VMEM)
+    dma = pltpu.SemaphoreType.DMA
+    out = pl.pallas_call(
+        functools.partial(kernel, n, nb),
+        out_shape=(
+            jax.ShapeDtypeStruct((T, HEADS * H), BF16),
+            jax.ShapeDtypeStruct((T, KV_HEADS * H), BF16),
+            jax.ShapeDtypeStruct((share, KV_HEADS * H), F32),
+        ),
+        in_specs=[vm] * 6 + [pl.BlockSpec(memory_space=pltpu.SMEM), vm],
+        out_specs=(vm, vm, vm),
+        scratch_shapes=[
+            pltpu.VMEM((n, T, R * H), BF16),
+            pltpu.VMEM((n, T, R * H), BF16),
+            pltpu.VMEM((n, T, H), BF16),
+            pltpu.VMEM((n, T, H), BF16),
+            pltpu.VMEM((n, T, win), BF16),
+            pltpu.VMEM((n, 8, T), F32),
+            pltpu.VMEM((n, 8, T), F32),
+            pltpu.VMEM((H, L), BF16),
+            pltpu.VMEM((win, L), BF16),
+            pltpu.VMEM((L, H), F32),
+            pltpu.VMEM((L, H), F32),
+            pltpu.VMEM((n, T, R * H), BF16),
+            pltpu.VMEM((n, T, H), BF16),
+            pltpu.VMEM((n, L, H), BF16),
+            pltpu.VMEM((win, H), F32),
+            pltpu.VMEM((n, share, H), BF16),
+            pltpu.VMEM((n, share, H), BF16),
+            pltpu.VMEM((n, share, H), BF16),
+            pltpu.VMEM((n, share, H), BF16),
+            pltpu.VMEM((n, T, R * H), BF16),
+            pltpu.VMEM((n, T, H), BF16),
+            dma((6, n)), dma((6, n)), dma((3, n)), dma((3, n)),
+            dma((n,)), dma((n,)), dma((n,)), dma((n,)),
+        ],
+        compiler_params=pltpu.CompilerParams(
+            collective_id=0, has_side_effects=True, vmem_limit_bytes=56 * 1024 * 1024
+        ),
+    )(
+        query_rows[0], key_rows[0], value_rows[0], attn_output[0], output_grad[0], log_norm[0],
+        slab_order, normed_input[0],
+    )
+    return out[0][None], out[1][None], out[2]
+
+
+def pick(*args):
+    n, nb = lax.axis_size("seq"), lax.axis_size("batch")
+    fits = n == KV_HEADS and n & (n - 1) == 0 and nb % 2 == 0 and args[0].shape[1] == 128
+    return by_heads(n, nb, *args) if fits else local(*args)
+
+
 def solution(mesh):
     placed = (
         P("batch", "seq", None),
@@ -111,7 +475,7 @@
         P("batch", "seq", None),
     )
     return jax.shard_map(
-        local,
+        pick,
         mesh=mesh,
         in_specs=placed,
         out_specs=(P("batch", "seq", None), P("batch", "seq", None), P("seq", None)),

time: 278 us -> 119 us (0.43)
  waiting for transfers between devices: 178 us -> 0 us
  Pallas kernels: 0 us -> 111 us
  local copies, waits for them, and re-layouts: 35.5 us -> 6.91 us
  matrix products: 24.2 us -> 0 us
  between operations: 14.9 us -> 1.29 us
  other arithmetic: 11.3 us -> 0 us
  blocking collectives: 9.51 us -> 0 us
  starting transfers between devices: 4.68 us -> 0 us
    pallas_call x0 -> x1, Pallas kernels: none -> 111 us  [by_heads(): pl.pallas_call(functools.partial(kernel, n, nb), out_shape=(jax.ShapeDtyp...]
    all_gather x3 -> x0, waiting for transfers between devices: 60.5 us -> none  [the longest x1 24.1 us: local(): lax.all_gather(value_sum.astype(jnp.bfloat16), 'seq', axis=0, tiled=True)]
    reduce_scatter x1 -> x0, waiting for transfers between devices: 41.3 us -> none  [local(): lax.psum_scatter(part_key.astype(jnp.bfloat16), 'seq', scatter_dimension=...]
    unnamed x7 -> x0, waiting for transfers between devices: 40.4 us -> none
    psum x1 -> x0, waiting for transfers between devices: 35.4 us -> none  [local(): lax.psum(rows_total.astype(jnp.bfloat16), 'batch').astype(jnp.float32)]
    dot_general x11 -> x0, matrix products: 24.2 us -> none  [the longest x2 6.83 us: block_terms(): jnp.einsum('tgrd,kgd->grtk', grads, value_block, preferred_element_type=j...]
    unnamed x1 -> x0, blocking collectives: 9.51 us -> none
    unnamed x29 -> x3, local copies, waits for them, and re-layouts: 15.3 us -> 6.91 us
  transfers between devices with their start and end apart: 7 -> 0, of which waited for: 6 -> 0; matrix products, arithmetic and copies ran while one was open for 18% -> 0% of each run, Pallas kernels for 0% -> 0%
where the time goes in v1:
time: 119 us
  Pallas kernels  111 us (93%)
  local copies, waits for them, and re-layouts  6.91 us (6%)
  between operations  1.29 us (1%)
    pallas_call x1, Pallas kernels, by_heads(): pl.pallas_call(functools.partial(kernel, n, nb), out_shape=(jax.ShapeDtyp...  111 us
    unnamed x3, local copies, waits for them, and re-layouts  6.91 us

profile of v1, /device:TPU:0, one launch (start us, length us, event | category | flops | bytes accessed | tf_op | source)
XLA Modules:
  0.0 118.9 jit_solution(2892944850484834398)
XLA Ops:
  1.3 110.7 %shard_map.103 = (bf16[128,2048]{1,0:T(8,128)(2,1)}, bf16[128,1024]{1,0:T(8,128)(2,1)}, f32[576,1024]{1,0:T(8,128)}) custom-call(bf16[128,2048]{1,0:T(8,128)(2,1)} %bitcast.11, bf16[128,1024]{1,0:T(8,128)(2,1)} %bitcast.15, bf16[128,1024]{1,0:T(8,128)(2,1)} %bitcast.16, bf16[128,2048]{1,0:T(8,128)(2,1)} %bitcast.12, bf16[128,2048]{1,0:T(8,128)(2,1)} %bitcast.13, ...), custom_call_target="tpu_custom_call" | custom-call | tf_op jit(solution)/shard_map/pallas_call | solution.py:416
  112.0 1.9 %copy.15 = bf16[1,128,2048]{2,1,0:T(8,128)(2,1)} copy(bf16[1,128,2048]{2,1,0:T(8,128)(2,1)} %bitcast.10) | data formatting | bytes 1048576
  113.8 1.7 %copy.16 = bf16[1,128,1024]{2,1,0:T(8,128)(2,1)} copy(bf16[1,128,1024]{2,1,0:T(8,128)(2,1)} %bitcast.14) | data formatting | bytes 524288
  115.5 3.4 %copy.17 = f32[576,1024]{1,0:T(8,128)} copy(f32[576,1024]{1,0:T(8,128)} %get-tuple-element.14) | data formatting | bytes 4718592

commit v2 on v1

--- a/solution.py
+++ b/solution.py
@@ -135,7 +135,7 @@
     gq_ref, gk_ref, gw_ref,
     qr, gr, kr, vr, xr, st_src, str_, kt, xt, dk_acc, dv_acc, dq_buf, dk_buf, dv_all,
     prod, up, cr, snd, tot, gq_in, gk_in,
-    in_send, in_recv, out_send, out_recv, zu_send, zu_recv, zc_recv, zd_send,
+    in_send, in_recv, out_send, out_recv, zu_send, zu_recv, zc_recv, zd_send, fw_send, loc, g_vm, o_vm,
 ):
     me = lax.axis_index("seq")
     b = lax.axis_index("batch")
@@ -201,10 +201,27 @@
         send_in(2, t).start()
         send_in(3, t).start()
 
+    owns = [
+        pltpu.make_async_copy(src, dst, loc.at[j])
+        for j, (src, dst) in enumerate((
+            (g_ref, g_vm),
+            (o_ref, o_vm),
+            (k_ref.at[:, cols(me, H)], kr.at[me]),
+            (v_ref.at[:, cols(me, H)], vr.at[me]),
+            (q_ref.at[:, cols(me, R * H)], qr.at[me]),
+            (g_ref.at[:, cols(me, R * H)], gr.at[me]),
+            (x_ref.at[:, pl.ds(xstart(me), win)], xr.at[me]),
+        ))
+    ]
+    for own in owns:
+        own.start()
+    for own in owns[:2]:
+        own.wait()
+
     lane = lax.broadcasted_iota(jnp.int32, (T, 128), 1)
     table = jnp.zeros((T, 128), F32)
     for h in range(HEADS):
-        part = g_ref[:, h * H:(h + 1) * H].astype(F32) * o_ref[:, h * H:(h + 1) * H].astype(F32)
+        part = g_vm[:, h * H:(h + 1) * H].astype(F32) * o_vm[:, h * H:(h + 1) * H].astype(F32)
         table = jnp.where(lane == h, jnp.sum(part, axis=1, keepdims=True), table)
     delta = jnp.transpose(table)
     base = jnp.full((8 - 2 * R, T), (order_ref[0, 0] * T).astype(F32))
@@ -217,11 +234,8 @@
     for t in range(1, n):
         send_in(4, t).start()
 
-    kr[me] = k_ref[:, cols(me, H)]
-    vr[me] = v_ref[:, cols(me, H)]
-    qr[me] = q_ref[:, cols(me, R * H)]
-    gr[me] = g_ref[:, cols(me, R * H)]
-    xr[me] = x_ref[:, pl.ds(xstart(me), win)]
+    for own in owns[2:]:
+        own.wait()
     str_[me] = st_src[me]
     dk_acc[...] = jnp.zeros_like(dk_acc)
     dv_acc[...] = jnp.zeros_like(dv_acc)
@@ -277,7 +291,8 @@
 
     dv_all[me] = dv_acc[...].astype(BF16)
     for t in range(1, n):
-        send_out(0, t).start()
+        if t == 1 or t % 2 == 0:
+            send_out(0, t).start()
     dk_buf[...] = (dk_acc[...] * SCALE).astype(BF16).reshape(dk_buf.shape)
     for kind in (1, 2):
         for t in range(1, n):
@@ -312,10 +327,20 @@
             src_ref=tot.at[c], dst_ref=cr.at[c], send_sem=zd_send.at[c], recv_sem=zc_recv.at[c],
             device_id=at(me, outer), device_id_type=MESH)
 
+    def forward(c):
+        head = xor(me, c, n)
+        return pltpu.make_async_remote_copy(
+            src_ref=dv_all.at[head], dst_ref=dv_all.at[head], send_sem=fw_send.at[c],
+            recv_sem=out_recv.at[0, c + 1], device_id=at(xor(me, jnp.int32(1), n), b), device_id_type=MESH)
+
     def go_up(c):
         @pl.when(c > 0)
         def _():
             send_out(0, c).wait_recv()
+
+        @pl.when(jnp.logical_and(c > 0, lax.rem(c, 2) == 0))
+        def _():
+            forward(c).start()
 
         prod[...] = jnp.dot(xt[...], dv_all[xor(me, c, n)], preferred_element_type=F32)
 
@@ -352,22 +377,22 @@
         def _():
             outward(c).start()
 
-        gw_ref[:, head] = tot[c].astype(F32)
-
-    lag = 2
+        gw_ref[:, head] = tot[c]
+
+    lag = jnp.where(is_mid, 2, n)
 
     def z_step(c, carry):
         @pl.when(c < n)
         def _():
             go_up(c)
 
-        @pl.when(c >= lag)
+        @pl.when(jnp.logical_and(c >= lag, c < lag + n))
         def _():
             go_down(c - lag)
 
         return carry
 
-    lax.fori_loop(0, n + lag, z_step, 0)
+    lax.fori_loop(0, 2 * n, z_step, 0)
 
     gk_ref[:, cols(me, H)] = dk_buf[me]
     gq_ref[:, cols(me, R * H)] = dq_buf[me]
@@ -385,8 +410,18 @@
     def drain(t, carry):
         for kind in range(6):
             send_in(kind, t).wait_send()
-        for kind in range(3):
+        for kind in (1, 2):
             send_out(kind, t).wait_send()
+        even = lax.rem(t, 2) == 0
+
+        @pl.when(jnp.logical_or(t == 1, even))
+        def _():
+            send_out(0, t).wait_send()
+
+        @pl.when(even)
+        def _():
+            forward(t).wait_send()
+
         return carry
 
     lax.fori_loop(1, n, drain, 0)
@@ -412,15 +447,16 @@
     L = n * T
     share, win = window(normed_input.shape[2], n)
     vm = pl.BlockSpec(memory_space=pltpu.VMEM)
+    hbm = pl.BlockSpec(memory_space=pl.ANY)
     dma = pltpu.SemaphoreType.DMA
     out = pl.pallas_call(
         functools.partial(kernel, n, nb),
         out_shape=(
             jax.ShapeDtypeStruct((T, HEADS * H), BF16),
             jax.ShapeDtypeStruct((T, KV_HEADS * H), BF16),
-            jax.ShapeDtypeStruct((share, KV_HEADS * H), F32),
+            jax.ShapeDtypeStruct((share, KV_HEADS * H), BF16),
         ),
-        in_specs=[vm] * 6 + [pl.BlockSpec(memory_space=pltpu.SMEM), vm],
+        in_specs=[hbm] * 5 + [vm, pl.BlockSpec(memory_space=pltpu.SMEM), hbm],
         out_specs=(vm, vm, vm),
         scratch_shapes=[
             pltpu.VMEM((n, T, R * H), BF16),
@@ -445,7 +481,9 @@
             pltpu.VMEM((n, T, R * H), BF16),
             pltpu.VMEM((n, T, H), BF16),
             dma((6, n)), dma((6, n)), dma((3, n)), dma((3, n)),
-            dma((n,)), dma((n,)), dma((n,)), dma((n,)),
+            dma((n,)), dma((n,)), dma((n,)), dma((n,)), dma((n,)), dma((7,)),
+            pltpu.VMEM((T, HEADS * H), BF16),
+            pltpu.VMEM((T, HEADS * H), BF16),
         ],
         compiler_params=pltpu.CompilerParams(
             collective_id=0, has_side_effects=True, vmem_limit_bytes=56 * 1024 * 1024
@@ -454,7 +492,7 @@
         query_rows[0], key_rows[0], value_rows[0], attn_output[0], output_grad[0], log_norm[0],
         slab_order, normed_input[0],
     )
-    return out[0][None], out[1][None], out[2]
+    return out[0][None], out[1][None], out[2].astype(F32)
 
 
 def pick(*args):

time: 119 us -> 87.5 us (0.74)
  Pallas kernels: 111 us -> 81.1 us
  local copies, waits for them, and re-layouts: 6.91 us -> 1.8 us
  other arithmetic: 0 us -> 3.02 us
    pallas_call x1, Pallas kernels: 111 us -> 81.1 us  [by_heads(): pl.pallas_call(functools.partial(kernel, n, nb), out_shape=(jax.ShapeDtyp...]
    unnamed x3 -> x6, local copies, waits for them, and re-layouts: 6.91 us -> 1.8 us
    convert_element_type x0 -> x1, other arithmetic: none -> 3.02 us  [by_heads(): return (out[0][None], out[1][None], out[2].astype(F32))]
where the time goes in v2:
time: 87.5 us; the launch traced here: 87.2 us
  Pallas kernels  81.1 us (93%)
  other arithmetic  3.02 us (3%)
  local copies, waits for them, and re-layouts  1.8 us (2%)
  between operations  1.3 us (1%)
    pallas_call x1, Pallas kernels, by_heads(): pl.pallas_call(functools.partial(kernel, n, nb), out_shape=(jax.ShapeDtyp...  81.1 us
    convert_element_type x1, other arithmetic, by_heads(): return (out[0][None], out[1][None], out[2].astype(F32))  3.02 us
    unnamed x6, local copies, waits for them, and re-layouts  1.8 us

profile of v2, /device:TPU:0, one launch (start us, length us, event | category | flops | bytes accessed | tf_op | source)
XLA Modules:
  0.0 87.2 jit_solution(5578278109091891996)
XLA Ops:
  1.3 81.1 %shard_map.103 = (bf16[128,2048]{1,0:T(8,128)(2,1)}, bf16[128,1024]{1,0:T(8,128)(2,1)}, bf16[576,1024]{1,0:T(8,128)(2,1)}) custom-call(bf16[128,2048]{1,0:T(8,128)(2,1)} %bitcast.11, bf16[128,1024]{1,0:T(8,128)(2,1)} %bitcast.15, bf16[128,1024]{1,0:T(8,128)(2,1)} %bitcast.16, bf16[128,2048]{1,0:T(8,128)(2,1)} %bitcast.12, bf16[128,2048]{1,0:T(8,128)(2,1)} %bitcast.13, ...), custom_call_target="tpu_custom_call" | custom-call | tf_op jit(solution)/shard_map/pallas_call | solution.py:452
  82.4 0.0 copy-start
  82.4 3.0 %convert_element_type.3 = f32[576,1024]{1,0:T(8,128)} convert(bf16[576,1024]{1,0:T(8,128)(2,1)} %get-tuple-element.8) | non-fusion elementwise | flops 589824 | bytes 3538944 | tf_op jit(solution)/shard_map/convert_element_type | solution.py:495
  85.4 0.0 copy-done
  85.4 0.0 copy-start.1
  85.4 0.8 copy.14
  86.2 0.3 copy-done.1
  86.5 0.7 copy.15
Async XLA Ops:
  82.4 3.0 %copy-start = (bf16[128,2048]{1,0:T(8,128)(2,1)S(1)}, bf16[128,2048]{1,0:T(8,128)(2,1)}, u32[]{:S(2)}) copy-start(bf16[128,2048]{1,0:T(8,128)(2,1)} %get-tuple-element.6) | copy-start | bytes 1572868
  85.4 1.1 %copy-start.1 = (bf16[128,1024]{1,0:T(8,128)(2,1)S(1)}, bf16[128,1024]{1,0:T(8,128)(2,1)}, u32[]{:S(2)}) copy-start(bf16[128,1024]{1,0:T(8,128)(2,1)} %get-tuple-element.7) | copy-start | bytes 786436
